TPU v7x, 32 devices: a whole 2x2x4 slice. The times are simulated.
32 devices in a mesh: grp: 4 (over z), mem: 8 (over y, x, core).
Axes of the slice: x: 2, y: 2, z: 4, core: 2. Of those that a mesh axis runs over, the one named last changes fastest.
Arguments:
- embeddings: bfloat16 [32768, 4096], P(('grp', 'mem')), may hold values from -6 to 6
- local_picks: int32 [4, 64], P('grp', 'mem'), may hold values from 0 to 1023
- second_picks: int32 [4, 16], P('grp'), may hold values from 0 to 63
- final_picks: int32 [16], replicated, may hold values from 0 to 63
Outputs:
- gain_table: float32 [64, 64], P('grp', 'mem')
- final_cover: float32 [32768], P(('grp', 'mem'))
Inputs may be any that keep to these rules, and one draw needn't show every extreme that they name: `local_picks`: entry (g, m * 8 + k) names a row among the 1024 points of device m of group g; repeats may occur. `second_picks`: candidate indices of the group, in greedy order; repeats may occur. `final_picks`: index g * 16 + t names group g's second-round pick t; repeats may occur.
All inputs are finite; a program needn't handle non-finite values.
Results may differ from a plain program's by a relative error of at most 0.0003.
Values may be sent and summed in bfloat16 or wider, within the bound.
A program may use at most 64 MiB of HBM per device.

v0:
```python
import jax
import jax.numpy as jnp
from jax import lax
from jax.sharding import PartitionSpec as P

D = 4096


def per_device(embeddings, local_picks, second_picks, final_picks):
    scaling = float(D) ** (-0.5)
    point_count = embeddings.shape[0]
    local_count = local_picks.shape[1]
    second_list = second_picks[0]
    member = lax.axis_index("mem")
    choose = (local_picks[0][:, None] == lax.iota(jnp.int32, point_count)[None, :]).astype(
        jnp.bfloat16
    )
    own_rows = jnp.dot(choose, embeddings, preferred_element_type=jnp.float32).astype(jnp.bfloat16)

    def similar(other_rows):
        dims = (((1,), (1,)), ((), ()))
        return (
            lax.dot_general(embeddings, other_rows, dims, preferred_element_type=jnp.float32)
            * scaling
        )

    candidates = lax.all_gather(own_rows, "mem", axis=0, tiled=True)
    similar_map = similar(candidates)
    cand_total = candidates.shape[0]
    pick_table = (second_list[:, None] == lax.iota(jnp.int32, cand_total)[None, :]).astype(
        jnp.bfloat16
    )
    winners = jnp.dot(pick_table, candidates, preferred_element_type=jnp.float32).astype(
        jnp.bfloat16
    )
    union_rows = lax.all_gather(winners, "grp", axis=0, tiled=True)
    final_table = (
        final_picks[:, None] == lax.iota(jnp.int32, union_rows.shape[0])[None, :]
    ).astype(jnp.bfloat16)
    final_rows = jnp.dot(final_table, union_rows, preferred_element_type=jnp.float32).astype(
        jnp.bfloat16
    )
    own_block = lax.dynamic_slice_in_dim(similar_map, member * local_count, local_count, 1)
    coverage = jnp.max(own_block, axis=1)
    chosen_cols = jnp.take(similar_map, second_list, axis=1)

    def greedy_step(cover_now, column):
        partial_value = jnp.sum(jnp.maximum(similar_map - cover_now[:, None], 0.0), axis=0)
        return (jnp.maximum(cover_now, column), partial_value)

    _, partials = lax.scan(greedy_step, coverage, chosen_cols.T)
    gain_table = lax.psum_scatter(partials, "mem", scatter_dimension=1, tiled=True) / point_count
    final_cover = jnp.max(similar(final_rows), axis=1)
    return (gain_table, final_cover)


def solution(mesh):
    placed = (P(("grp", "mem"), None), P("grp", "mem"), P("grp", None), P())
    return jax.shard_map(
        per_device,
        mesh=mesh,
        in_specs=placed,
        out_specs=(P("grp", "mem"), P(("grp", "mem"))),
        check_vma=False,
    )
```

profile of v0, /device:TPU:0, one launch (start us, length us, event | category | flops | bytes accessed | tf_op | source)
XLA Modules:
  0.0 75.5 jit_solution(6943562138550951512)
XLA Ops:
  0.6 1.2 %dynamic-slice.4 = u32[1]{0:T(128)} dynamic-slice(u32[32]{0:T(128)} %constant.50, u32[]{:T(128)S(6)} %add.27), dynamic_slice_sizes={1} | dynamic-slice | bytes 12
  2.5 0.7 compare_and_fusion
  3.2 0.7 fusion.7
  3.9 4.8 %convolution_convert_fusion.2 = bf16[8,4096]{1,0:T(8,128)(2,1)S(1)} fusion(bf16[1024,4096]{1,0:T(8,128)(2,1)} %param.6, s32[8]{0:T(128)} %bitcast.25), kind=kOutput, calls=%fused_computation.5 | convolution fusion | flops 67149824 | bytes 8454176 | tf_op jit(solution)/shard_map/dot_general | solution.py:18
  8.7 11.3 %all_gather.6 = bf16[64,4096]{1,0:T(8,128)(2,1)S(1)} all-gather(bf16[8,4096]{1,0:T(8,128)(2,1)S(1)} %convolution_convert_fusion.2), channel_id=1, replica_groups=mesh['grp'=4,'mem'=8] {'mem'}, dimensions={0}, use_global_device_ids=true | all-gather | bytes 589824 | tf_op jit(solution)/shard_map/all_gather | solution.py:27
  20.0 0.2 convolution_convert_fusion.1
  20.3 2.7 %convolution_multiply_fusion = f32[64,1024]{1,0:T(8,128)S(1)} fusion(bf16[64,4096]{1,0:T(8,128)(2,1)S(1)} %all_gather.6, bf16[1024,4096]{1,0:T(8,128)(2,1)S(1)} %copy-done), kind=kOutput, calls=%fused_computation.6 | convolution fusion | flops 536936448 | bytes 9175040 | tf_op jit(solution)/shard_map/dot_general | solution.py:23
  23.0 0.6 gather_fusion
  23.5 0.1 broadcast_select_fusion
  23.6 0.2 copy.8
  23.8 4.8 %while.12 = (s32[]{:T(128)}, f32[1024]{0:T(1024)S(1)}, f32[16,64]{1,0:T(8,128)S(1)}, f32[16,1024]{1,0:T(8,128)S(1)}, f32[1024,64]{1,0:T(8,128)S(1)}, /*index=5*/s32[]{:T(128)}, s32[]{:T(128)}) while((s32[]{:T(128)}, f32[1024]{0:T(1024)S(1)}, f32[16,64]{1,0:T(8,128)S(1)}, f32[16,1024]{1,0:T(8,128)S(1)}, f32[1024,64]{1,0:T(8,128)S(1)}, ...), condition=%wide.region_3.4_spmd, body=%wide.region_1.0_spmd.sunk | while | flops 197570 | bytes 287581 | solution.py:51
  23.8 0.2 maximum_reduce_fusion.2
  24.1 0.2 maximum_reduce_fusion.2
  24.4 0.2 maximum_reduce_fusion.2
  24.7 0.2 maximum_reduce_fusion.2
  25.0 0.2 maximum_reduce_fusion.2
  25.3 0.2 maximum_reduce_fusion.2
  25.6 0.2 maximum_reduce_fusion.2
  25.9 0.2 maximum_reduce_fusion.2
  26.2 0.2 maximum_reduce_fusion.2
  26.5 0.2 maximum_reduce_fusion.2
  26.8 0.2 maximum_reduce_fusion.2
  27.1 0.2 maximum_reduce_fusion.2
  27.5 0.2 maximum_reduce_fusion.2
  27.8 0.2 maximum_reduce_fusion.2
  28.1 0.2 maximum_reduce_fusion.2
  28.4 0.2 maximum_reduce_fusion.2
  28.7 0.1 copy.9
  28.7 23.6 %all-reduce = f32[16,64]{0,1:T(8,128)S(1)} all-reduce(f32[16,64]{0,1:T(8,128)S(1)} %copy.9), channel_id=2, replica_groups=mesh['grp'=4,'mem'=8] {'mem'}, use_global_device_ids=true, to_apply=%region_4.5.clone | all-reduce | flops 1024 | bytes 8192
  52.3 0.6 dynamic-slice_multiply_fusion
  52.9 16.2 %all_gather.7 = bf16[64,4096]{1,0:T(8,128)(2,1)S(1)} all-gather(bf16[16,4096]{1,0:T(8,128)(2,1)S(1)} %convolution_convert_fusion.1), channel_id=1, replica_groups=mesh['grp'=4,'mem'=8] {'grp'}, dimensions={0}, use_global_device_ids=true | all-gather | bytes 655360 | tf_op jit(solution)/shard_map/all_gather | solution.py:36
  69.1 6.4 %fusion.2 = f32[1024]{0:T(1024)} fusion(bf16[1024,4096]{1,0:T(8,128)(2,1)} %param.6, bf16[64,4096]{1,0:T(8,128)(2,1)S(1)} %all_gather.7, s32[16]{0:T(128)S(1)} %copy-done.1), kind=kOutput, calls=%fused_computation.9 | convolution fusion | flops 142704640 | bytes 8917056 | tf_op jit(solution)/shard_map/dot_general | solution.py:23
  (57 shorter events, 0.9 us)
Async XLA Ops:
  0.6 19.4 %copy-start.2 = (s32[1,16]{1,0:T(1,128)S(1)}, s32[1,16]{1,0:T(1,128)}, u32[]{:S(2)}) copy-start(s32[1,16]{1,0:T(1,128)} %param.8) | copy-start | bytes 196
  3.9 16.4 %copy-start = (bf16[1024,4096]{1,0:T(8,128)(2,1)S(1)}, bf16[1024,4096]{1,0:T(8,128)(2,1)}, u32[]{:S(2)}) copy-start(bf16[1024,4096]{1,0:T(8,128)(2,1)} %param.6) | copy-start | bytes 25165828
  20.3 48.9 %copy-start.1 = (s32[16]{0:T(128)S(1)}, s32[16]{0:T(128)}, u32[]{:S(2)}) copy-start(s32[16]{0:T(128)} %param.9) | copy-start | bytes 196
where the time goes:
time: 75.8 us; the launch traced here: 75.5 us
  blocking collectives  51.1 us (67%)
  matrix products  14.1 us (19%)
  other arithmetic  5.58 us (7%)
  local copies, waits for them, and re-layouts  2.9 us (4%)
  between operations  1.36 us (2%)
    unnamed x1, blocking collectives  23.6 us
    all_gather x1, blocking collectives, per_device(): union_rows = lax.all_gather(winners, 'grp', axis=0, tiled=True)  16.2 us
    all_gather x1, blocking collectives, per_device(): candidates = lax.all_gather(own_rows, 'mem', axis=0, tiled=True)  11.3 us
    dot_general x2, matrix products, similar(): lax.dot_general(embeddings, other_rows, dims, preferred_element_type=jnp....  9.06 us
    dot_general x1, matrix products, per_device(): jnp.dot(choose, embeddings, preferred_element_type=jnp.float32)  4.78 us
    reduce_sum x16, other arithmetic, greedy_step(): jnp.sum(jnp.maximum(similar_map - cover_now[:, None], 0.0), axis=0)  3.49 us

commit v1 on v0

--- a/solution.py
+++ b/solution.py
@@ -4,6 +4,12 @@
 from jax.sharding import PartitionSpec as P
 
 D = 4096
+
+
+def joined_along(pieces, dim):
+    lengths = list(pieces.shape[1:])
+    lengths[dim] *= pieces.shape[0]
+    return jnp.moveaxis(pieces, 0, dim).reshape(lengths)
 
 
 def per_device(embeddings, local_picks, second_picks, final_picks):
@@ -33,7 +39,19 @@
     winners = jnp.dot(pick_table, candidates, preferred_element_type=jnp.float32).astype(
         jnp.bfloat16
     )
-    union_rows = lax.all_gather(winners, "grp", axis=0, tiled=True)
+    count = lax.axis_size("grp")
+    pairs = [(i, (i + 1) % count) for i in range(count)]
+    back = [(b, a) for a, b in pairs]
+    lower, upper = ([], [])
+    for step in range(count - 1):
+        if step % 2 == 0:
+            lower.append(lax.ppermute(lower[-1] if lower else winners, "grp", pairs))
+        else:
+            upper.append(lax.ppermute(upper[-1] if upper else winners, "grp", back))
+    parts = jnp.stack([*lower[::-1], winners, *upper])
+    shift = lax.axis_index("grp") - len(lower)
+    parts = parts[(jnp.arange(count) - shift) % count]
+    union_rows = joined_along(parts, 0)
     final_table = (
         final_picks[:, None] == lax.iota(jnp.int32, union_rows.shape[0])[None, :]
     ).astype(jnp.bfloat16)

time: 75.8 us -> 62.3 us (0.82)
  blocking collectives: 51.1 us -> 34.9 us
  starting transfers between devices: 0 us -> 3.93 us
  other arithmetic: 5.58 us -> 4.36 us
    all_gather x1 -> x0, blocking collectives: 16.2 us -> none  [per_device(): union_rows = lax.all_gather(winners, 'grp', axis=0, tiled=True)]
    ppermute x0 -> x3, starting transfers between devices: none -> 3.93 us  [the longest x1 2.25 us: per_device(): upper.append(lax.ppermute(upper[-1] if upper else winners, 'grp', back))]
  transfers between devices with their start and end apart: 0 -> 3, of which waited for: 0 -> 0; matrix products, arithmetic and copies ran while one was open for 0% -> 15% of each run, Pallas kernels for 0% -> 0%
where the time goes in v1:
time: 62.3 us; the launch traced here: 62 us
  blocking collectives  34.9 us (56%)
  matrix products  14.1 us (23%)
  other arithmetic  4.36 us (7%)
  starting transfers between devices  3.93 us (6%)
  local copies, waits for them, and re-layouts  2.82 us (5%)
  between operations  1.45 us (2%)
    unnamed x1, blocking collectives  23.5 us
    all_gather x1, blocking collectives, per_device(): candidates = lax.all_gather(own_rows, 'mem', axis=0, tiled=True)  11.5 us
    dot_general x2, matrix products, similar(): lax.dot_general(embeddings, other_rows, dims, preferred_element_type=jnp....  9.06 us
    dot_general x1, matrix products, per_device(): jnp.dot(choose, embeddings, preferred_element_type=jnp.float32)  4.78 us
    reduce_sum x16, other arithmetic, greedy_step(): jnp.sum(jnp.maximum(similar_map - cover_now[:, None], 0.0), axis=0)  3.49 us
    ppermute x1, starting transfers between devices, per_device(): upper.append(lax.ppermute(upper[-1] if upper else winners, 'grp', back))  2.25 us
    ppermute x2, starting transfers between devices, per_device(): lower.append(lax.ppermute(lower[-1] if lower else winners, 'grp', pairs))  1.69 us
  transfers between devices with their start and end apart: 3, of which 0 were waited for; matrix products, arithmetic and copies ran while one was open for 15% of the time, Pallas kernels for 0%

profile of v1, /device:TPU:0, one launch (start us, length us, event | category | flops | bytes accessed | tf_op | source)
XLA Modules:
  0.0 62.0 jit_solution(16023083969853855764)
XLA Ops:
  0.7 4.8 %convolution_convert_fusion.2 = bf16[8,4096]{1,0:T(8,128)(2,1)S(1)} fusion(bf16[1024,4096]{1,0:T(8,128)(2,1)} %param.6, s32[8]{0:T(128)} %bitcast.39), kind=kOutput, calls=%fused_computation.6 | convolution fusion | flops 67149824 | bytes 8454176 | tf_op jit(solution)/shard_map/dot_general | solution.py:24
  5.4 11.5 %all_gather.3 = bf16[64,4096]{1,0:T(8,128)(2,1)S(1)} all-gather(bf16[8,4096]{1,0:T(8,128)(2,1)S(1)} %convolution_convert_fusion.2), channel_id=1, replica_groups=mesh['grp'=4,'mem'=8] {'mem'}, dimensions={0}, use_global_device_ids=true | all-gather | bytes 589824 | tf_op jit(solution)/shard_map/all_gather | solution.py:33
  16.9 0.2 convolution_convert_fusion.1
  17.1 1.6 %collective-permute-start = (bf16[16,4096]{1,0:T(8,128)(2,1)S(1)}, bf16[16,4096]{1,0:T(8,128)(2,1)S(1)}, u32[]{:S(2)}, u32[]{:S(2)}) collective-permute-start(bf16[16,4096]{1,0:T(8,128)(2,1)S(1)} %convolution_convert_fusion.1), channel_id=1, source_target_pairs={{0,8},{8,16},{16,24},{24,0},{1,9},{9,17},{17,25},{25,1},{2,10},{10... | collective-permute-start | bytes 393224 | tf_op jit(solution)/shard_map/ppermute | solution.py:48
  18.8 2.2 %collective-permute-start.2 = (bf16[16,4096]{1,0:T(8,128)(2,1)S(1)}, bf16[16,4096]{1,0:T(8,128)(2,1)S(1)}, u32[]{:S(2)}, u32[]{:S(2)}) collective-permute-start(bf16[16,4096]{1,0:T(8,128)(2,1)S(1)} %convolution_convert_fusion.1), channel_id=1, source_target_pairs={{8,0},{16,8},{24,16},{0,24},{9,1},{17,9},{25,17},{1,25},{10,2},{18... | collective-permute-start | bytes 393224 | tf_op jit(solution)/shard_map/ppermute | solution.py:50
  21.0 2.7 %convolution_multiply_fusion = f32[64,1024]{1,0:T(8,128)S(1)} fusion(bf16[64,4096]{1,0:T(8,128)(2,1)S(1)} %all_gather.3, bf16[1024,4096]{1,0:T(8,128)(2,1)S(1)} %bitcast.29), kind=kOutput, calls=%fused_computation.7 | convolution fusion | flops 536936448 | bytes 9175040 | tf_op jit(solution)/shard_map/dot_general | solution.py:29
  23.8 0.2 copy.8
  24.0 0.6 gather_fusion
  24.6 0.1 broadcast_select_fusion
  24.7 4.8 %while.12 = (s32[]{:T(128)}, f32[1024]{0:T(1024)S(1)}, f32[16,64]{1,0:T(8,128)S(1)}, f32[16,1024]{1,0:T(8,128)S(1)}, f32[1024,64]{1,0:T(8,128)S(1)}, /*index=5*/s32[]{:T(128)}, s32[]{:T(128)}) while((s32[]{:T(128)}, f32[1024]{0:T(1024)S(1)}, f32[16,64]{1,0:T(8,128)S(1)}, f32[16,1024]{1,0:T(8,128)S(1)}, f32[1024,64]{1,0:T(8,128)S(1)}, ...), condition=%wide.region_3.4_spmd, body=%wide.region_1.3_spmd.sunk | while | flops 197570 | bytes 287573 | solution.py:69
  24.7 0.2 maximum_reduce_fusion.2
  25.0 0.2 maximum_reduce_fusion.2
  25.3 0.2 maximum_reduce_fusion.2
  25.6 0.2 maximum_reduce_fusion.2
  25.9 0.2 maximum_reduce_fusion.2
  26.2 0.2 maximum_reduce_fusion.2
  26.5 0.2 maximum_reduce_fusion.2
  26.8 0.2 maximum_reduce_fusion.2
  27.1 0.2 maximum_reduce_fusion.2
  27.4 0.2 maximum_reduce_fusion.2
  27.7 0.2 maximum_reduce_fusion.2
  28.0 0.2 maximum_reduce_fusion.2
  28.3 0.2 maximum_reduce_fusion.2
  28.6 0.2 maximum_reduce_fusion.2
  28.9 0.2 maximum_reduce_fusion.2
  29.2 0.2 maximum_reduce_fusion.2
  29.6 0.1 copy.9
  29.7 0.6 dynamic-slice.4
  30.9 23.5 %all-reduce = f32[16,64]{0,1:T(8,128)S(1)} all-reduce(f32[16,64]{0,1:T(8,128)S(1)} %copy.9), channel_id=2, replica_groups=mesh['grp'=4,'mem'=8] {'mem'}, use_global_device_ids=true, to_apply=%region_4.5.clone | all-reduce | flops 1024 | bytes 8192
  54.4 0.6 dynamic-slice_multiply_fusion
  55.1 0.6 gather_fusion.1
  55.6 6.4 %fusion.2 = f32[1024]{0:T(1024)} fusion(bf16[1024,4096]{1,0:T(8,128)(2,1)} %param.6, bf16[64,4096]{1,0:T(8,128)(2,1)S(1)} %bitcast.32, s32[16]{0:T(128)S(1)} %copy-done), kind=kOutput, calls=%fused_computation.10 | convolution fusion | flops 142704640 | bytes 8917056 | tf_op jit(solution)/shard_map/dot_general | solution.py:29
  (71 shorter events, 1.1 us)
Async XLA Ops:
  0.6 20.4 %slice-start = ((s8[8388608]{0:T(1024)(128)(4,1)}), s8[4194304]{0:T(1024)(128)(4,1)S(1)}, s32[]{:S(2)}) async-start(s8[8388608]{0:T(1024)(128)(4,1)} %bitcast.28), calls=%async_computation | async-start | bytes 8388608
  0.6 16.3 %copy-start.1 = (s32[1,16]{1,0:T(1,128)S(1)}, s32[1,16]{1,0:T(1,128)}, u32[]{:S(2)}) copy-start(s32[1,16]{1,0:T(1,128)} %param.8) | copy-start | bytes 196
  0.7 20.4 %slice-start.1 = ((s8[8388608]{0:T(1024)(128)(4,1)}), s8[4194304]{0:T(1024)(128)(4,1)S(1)}, s32[]{:S(2)}) async-start(s8[8388608]{0:T(1024)(128)(4,1)} %bitcast.28), calls=%async_computation.1 | async-start | bytes 8388608
  17.1 12.3 %collective-permute-start = (bf16[16,4096]{1,0:T(8,128)(2,1)S(1)}, bf16[16,4096]{1,0:T(8,128)(2,1)S(1)}, u32[]{:S(2)}, u32[]{:S(2)}) collective-permute-start(bf16[16,4096]{1,0:T(8,128)(2,1)S(1)} %convolution_convert_fusion.1), channel_id=1, source_target_pairs={{0,8},{8,16},{16,24},{24,0},{1,9},{9,17},{17,25},{25,1},{2,10},{10... | collective-permute-start | bytes 393224 | tf_op jit(solution)/shard_map/ppermute | solution.py:48
  18.8 36.2 %collective-permute-start.2 = (bf16[16,4096]{1,0:T(8,128)(2,1)S(1)}, bf16[16,4096]{1,0:T(8,128)(2,1)S(1)}, u32[]{:S(2)}, u32[]{:S(2)}) collective-permute-start(bf16[16,4096]{1,0:T(8,128)(2,1)S(1)} %convolution_convert_fusion.1), channel_id=1, source_target_pairs={{8,0},{16,8},{24,16},{0,24},{9,1},{17,9},{25,17},{1,25},{10,2},{18... | collective-permute-start | bytes 393224 | tf_op jit(solution)/shard_map/ppermute | solution.py:50
  21.0 8.6 %copy-start.2 = (u32[32]{0:T(128)S(1)}, u32[32]{0:T(128)}, u32[]{:S(2)}) copy-start(u32[32]{0:T(128)} %constant.73) | copy-start | bytes 388
  21.0 34.6 %copy-start = (s32[16]{0:T(128)S(1)}, s32[16]{0:T(128)}, u32[]{:S(2)}) copy-start(s32[16]{0:T(128)} %param.9) | copy-start | bytes 196
  29.5 25.5 %collective-permute-start.1 = (bf16[16,4096]{1,0:T(8,128)(2,1)S(1)}, bf16[16,4096]{1,0:T(8,128)(2,1)S(1)}, u32[]{:S(2)}, u32[]{:S(2)}) collective-permute-start(bf16[16,4096]{1,0:T(8,128)(2,1)S(1)} %collective-permute-done), channel_id=1, source_target_pairs={{0,8},{8,16},{16,24},{24,0},{1,9},{9,17},{17,25},{25,1},{2,10},{10... | collective-permute-start | bytes 393224 | tf_op jit(solution)/shard_map/ppermute | solution.py:48
